TPU v7x, 32 devices: a whole 2x2x4 slice. The times are simulated.
32 devices in a mesh: grp: 8 (over y, x, core), wide: 4 (over z).
Axes of the slice: x: 2, y: 2, z: 4, core: 2. Of those that a mesh axis runs over, the one named last changes fastest.
Arguments:
- gradient: bfloat16 [8, 4, 16, 4096], P('grp', 'wide'), may hold values from -6 to 6
- residual: float32 [8, 4, 16, 4096], P('grp', 'wide'), may hold values from -4 to 4
- selected: int32 [8, 4, 4, 32], P('grp', 'wide'), may hold values from 0 to 127, as said below
- counts: int32 [8, 4, 4], P('grp', 'wide'), may hold values from 1 to 32, as said below
Outputs:
- update: float32 [4, 4, 4096], P('wide')
- new_residual: float32 [8, 4, 16, 4096], P('grp', 'wide')
Inputs may be any that keep to these rules, and one draw needn't show every extreme that they name: `selected`: for each device and shard, 32 distinct block numbers of that shard; entries at or past the count are ignored. `counts`: one shard has 32 on every device; every device has at most one other shard at 32, the rest at most 16.
All inputs are finite; a program needn't handle non-finite values.
Results may differ from a plain program's by a relative error of at most 0.0003.
Values sent between devices are 32-bit elements; how exact they have to be, the bound alone decides.
No kernel may reach another device: no remote copies, remote signals or barrier semaphores. Data moves between devices by JAX's collectives and lax.ppermute only.
A program may use at most 64 MiB of HBM per device.

v0:
```python
import jax
import jax.numpy as jnp
from jax import lax
from jax.sharding import PartitionSpec as P


def body(gradient, residual, selected, counts):
    shards = lax.axis_size("wide")
    groups = lax.axis_size("grp")
    rows = gradient.shape[2]
    width = gradient.shape[3]
    block_len = 128
    own_rows = rows // shards
    own_blocks = own_rows * width // block_len
    slots = selected.shape[3]
    accumulated = gradient[0, 0].astype(jnp.float32) + residual[0, 0]
    blocks = accumulated.reshape(shards, own_blocks, block_len)
    picks = selected[0, 0]
    used = counts[0, 0]
    block_ids = jnp.arange(own_blocks, dtype=jnp.int32)
    one_hot = (picks[:, :, None] == block_ids).astype(jnp.float32)
    valid = (jnp.arange(slots, dtype=jnp.int32)[None, :] < used[:, None]).astype(jnp.float32)
    mask = jnp.einsum("wk,wkb->wb", valid, one_hot, precision=lax.Precision.HIGHEST)
    new_residual = (blocks * (1.0 - mask[..., None])).reshape(1, 1, rows, width)
    chosen = (
        jnp.einsum("wkb,wbc->wkc", one_hot, blocks, precision=lax.Precision.HIGHEST)
        * valid[..., None]
    )
    chosen_ids = picks.astype(jnp.float32)
    arrived, arrived_ids = (
        lax.all_to_all(chosen, "wide", split_axis=0, concat_axis=0, tiled=True),
        lax.all_to_all(chosen_ids, "wide", split_axis=0, concat_axis=0, tiled=True),
    )
    arrived_hot = (arrived_ids[:, :, None] == block_ids.astype(jnp.float32)).astype(jnp.float32)
    partial_sum = jnp.einsum("skb,skc->bc", arrived_hot, arrived, precision=lax.Precision.HIGHEST)
    summed = lax.psum(partial_sum, "grp")
    update = (summed / groups).reshape(1, own_rows, width)
    return (update, new_residual)


def solution(mesh):
    return jax.shard_map(
        body,
        mesh=mesh,
        in_specs=(
            P("grp", "wide", None, None),
            P("grp", "wide", None, None),
            P("grp", "wide", None, None),
            P("grp", "wide", None),
        ),
        out_specs=(P("wide", None, None), P("grp", "wide", None, None)),
        check_vma=False,
    )
```

profile of v0, /device:TPU:0, one launch (start us, length us, event | category | flops | bytes accessed | tf_op | source)
XLA Modules:
  0.0 91.7 jit_solution(3083365458631421438)
XLA Ops:
  7.2 1.3 %convert_element_type.35 = f32[1,1,4,32]{3,2,1,0:T(4,128)} convert(s32[1,1,4,32]{3,2,1,0:T(4,128)} %param.6) | non-fusion elementwise | flops 128 | bytes 1024 | tf_op jit(solution)/shard_map/convert_element_type | solution.py:29
  8.4 6.3 %all-to-all-start = ((f32[4,1,32]{2,1,0:T(1,128)}), f32[4,1,32]{2,1,0:T(1,128)S(1)}, u32[]{:S(2)}, u32[]{:S(2)}) async-start(f32[4,1,32]{2,1,0:T(1,128)} %bitcast.1), calls=%async_computation | async-start | bytes 4096 | tf_op jit(solution)/shard_map/all_to_all | solution.py:32
  14.8 0.0 copy-start.3
  14.8 0.7 copy-done.3
  15.4 0.1 fusion.8
  15.5 0.0 copy-start.2
  15.5 0.7 copy-done.2
  16.2 0.2 fusion
  16.4 0.1 mul.21
  16.5 0.0 copy-start
  16.5 0.0 copy-start.1
  16.5 0.1 mul.22
  16.6 0.9 copy-done
  17.5 0.0 copy-done.1
  17.5 0.7 fusion.9
  18.3 0.9 convolution_multiply_fusion
  19.2 1.1 %all-to-all-done = f32[4,1,32]{2,1,0:T(1,128)S(1)} async-done(((f32[4,1,32]{2,1,0:T(1,128)}), f32[4,1,32]{2,1,0:T(1,128)S(1)}, u32[]{:S(2)}, u32[]{:S(2)}) %all-to-all-start) | async-done | bytes 544 | tf_op jit(solution)/shard_map/all_to_all | solution.py:32
  20.3 4.0 %all-to-all-start.1 = ((f32[4,32,128]{2,1,0:T(8,128)}), f32[4,32,128]{2,1,0:T(8,128)S(1)}, u32[]{:S(2)}, u32[]{:S(2)}) async-start(f32[4,32,128]{2,1,0:T(8,128)} %convolution_multiply_fusion), calls=%async_computation.1 | async-start | bytes 131072 | tf_op jit(solution)/shard_map/all_to_all | solution.py:31
  24.3 0.0 all-reduce.2.cloned.1.call-start
  24.3 5.7 %all-to-all-done.1 = f32[4,32,128]{2,1,0:T(8,128)S(1)} async-done(((f32[4,32,128]{2,1,0:T(8,128)}), f32[4,32,128]{2,1,0:T(8,128)S(1)}, u32[]{:S(2)}, u32[]{:S(2)}) %all-to-all-start.1) | async-done | bytes 65568 | tf_op jit(solution)/shard_map/all_to_all | solution.py:31
  30.1 0.9 %convolution_bitcast_fusion = f32[128,128]{1,0:T(8,128)} fusion(f32[4,32,128]{2,1,0:T(8,128)S(1)} %all-to-all-done.1, f32[128]{0:T(128)S(1)} %iota_convert_fusion, f32[4,32]{1,0:T(4,128)S(1)} %bitcast.16), kind=kOutput, calls=%fused_computation | convolution fusion | flops 25182208 | bytes 132096 | tf_op jit(solution)/shard_map/skb,skc->bc/dot_general | solution.py:35
  31.0 0.0 all-reduce.2.cloned.1.call-update
  31.0 52.4 %all-reduce.2.cloned.1.call-done = f32[128,128]{1,0:T(8,128)} async-done(((f32[128,128]{1,0:T(8,128)}), f32[128,128]{1,0:T(8,128)}) %all-reduce.2.cloned.1.call-update) | async-done | bytes 65552 | tf_op jit(solution)/shard_map/psum | solution.py:36
  83.4 0.8 broadcast_multiply_fusion
  84.2 0.7 reshape.63
  (3 shorter events, 0.1 us)
Async XLA Ops:
  8.4 11.9 %all-to-all-start = ((f32[4,1,32]{2,1,0:T(1,128)}), f32[4,1,32]{2,1,0:T(1,128)S(1)}, u32[]{:S(2)}, u32[]{:S(2)}) async-start(f32[4,1,32]{2,1,0:T(1,128)} %bitcast.1), calls=%async_computation | async-start | bytes 4096 | tf_op jit(solution)/shard_map/all_to_all | solution.py:32
  14.8 0.7 copy-start.3
  15.5 0.7 copy-start.2
  16.5 1.0 %copy-start = (f32[1,1,16,4096]{3,2,1,0:T(8,128)S(1)}, f32[1,1,16,4096]{3,2,1,0:T(8,128)}, u32[]{:S(2)}) copy-start(f32[1,1,16,4096]{3,2,1,0:T(8,128)} %param.5) | copy-start | bytes 786436
  16.5 1.0 %copy-start.1 = (bf16[1,1,16,4096]{3,2,1,0:T(8,128)(2,1)S(1)}, bf16[1,1,16,4096]{3,2,1,0:T(8,128)(2,1)}, u32[]{:S(2)}) copy-start(bf16[1,1,16,4096]{3,2,1,0:T(8,128)(2,1)} %param.4) | copy-start | bytes 393220
  20.3 9.7 %all-to-all-start.1 = ((f32[4,32,128]{2,1,0:T(8,128)}), f32[4,32,128]{2,1,0:T(8,128)S(1)}, u32[]{:S(2)}, u32[]{:S(2)}) async-start(f32[4,32,128]{2,1,0:T(8,128)} %convolution_multiply_fusion), calls=%async_computation.1 | async-start | bytes 131072 | tf_op jit(solution)/shard_map/all_to_all | solution.py:31
  24.3 59.1 %all-reduce.2.cloned.1.call-start = ((), (), s32[]{:S(2)}) async-start(), calls=%async_computation.2 | async-start | bytes 131072 | tf_op jit(solution)/shard_map/psum | solution.py:36
Sparse Core Ops, SparseCore 0:
  31.1 52.2 all-reduce.1
where the time goes:
time: 92.1 us; the launch traced here: 91.7 us
  waiting for transfers between devices  59.3 us (64%)
  between operations  14.1 us (15%)
  starting transfers between devices  10.3 us (11%)
  local copies, waits for them, and re-layouts  3.13 us (3%)
  other arithmetic  2.93 us (3%)
  matrix products  2.05 us (2%)
    psum x1, waiting for transfers between devices, body(): summed = lax.psum(partial_sum, 'grp')  52.4 us
    all_to_all x1, starting transfers between devices, body(): lax.all_to_all(chosen_ids, 'wide', split_axis=0, concat_axis=0, tiled=True)  6.35 us
    all_to_all x1, waiting for transfers between devices, body(): lax.all_to_all(chosen, 'wide', split_axis=0, concat_axis=0, tiled=True)  5.74 us
    all_to_all x1, starting transfers between devices, body(): lax.all_to_all(chosen, 'wide', split_axis=0, concat_axis=0, tiled=True)  3.96 us
    unnamed x8, local copies, waits for them, and re-layouts  2.25 us
  transfers between devices with their start and end apart: 3, of which 3 were waited for; matrix products, arithmetic and copies ran while one was open for 2% of the time, Pallas kernels for 0%

commit v1 on v0

v1 whole, which is shorter than its diff:
```python
import jax
import jax.numpy as jnp
from jax import lax
from jax.experimental import pallas as pl
from jax.experimental.pallas import tpu as pltpu
from jax.sharding import PartitionSpec as P

LANES = 128
PAD = 8


def is_pow2(n):
    return n & (n - 1) == 0


def fill_blocks(grad, res, acc):
    for c in range(acc.shape[0]):
        at = pl.ds(c * LANES, LANES)
        acc[c] = grad[:, at].astype(jnp.float32) + res[:, at]


def pick_call(grad, res, sel, cnt, info, shards, own_rows, by_xor):
    rows, width = grad.shape
    cols = width // LANES
    slots = sel.shape[1]
    per = LANES // slots

    def kernel(info_s, cnt_s, sel_s, sel_v, grad_v, res_v, *rest):
        outs, acc = rest[:-1], rest[-1]
        fill_blocks(grad_v, res_v, acc)
        me = info_s[0]
        lane = lax.broadcasted_iota(jnp.int32, (1, LANES), 1)

        def pack(shard, off, put):
            for k in range(slots):
                b = sel_s[shard, k]
                row = shard * own_rows + b // cols
                put(k, 1, acc[b % cols, pl.ds(row, 1), :])
            ids = sel_v[pl.ds(shard, 1), :]
            ids = (ids % cols) * own_rows + ids // cols
            ids = jnp.concatenate([ids] * per, axis=1)
            keep = (lane // slots == off) & (lane % slots < cnt_s[shard])
            ids = jnp.where(keep, ids, -1).astype(jnp.float32)
            put(slots, PAD, jnp.broadcast_to(ids, (PAD, LANES)))

        if by_xor:
            for j in range(shards):

                def put(at, n, value, out=outs[j]):
                    out[at : at + n, :] = value

                pack(me ^ j, j % per, put)
        else:
            def step(j, carry):
                def put(at, n, value):
                    outs[0][j, at : at + n, :] = value

                pack(j, me % per, put)
                return carry

            lax.fori_loop(0, shards, step, 0)

    smem = pl.BlockSpec(memory_space=pltpu.SMEM)
    vmem = pl.BlockSpec(memory_space=pltpu.VMEM)
    size = (slots + PAD, LANES)
    shapes = [jax.ShapeDtypeStruct(size, jnp.float32)] * shards
    if not by_xor:
        shapes = [jax.ShapeDtypeStruct((shards,) + size, jnp.float32)]
    return pl.pallas_call(
        kernel,
        out_shape=shapes,
        in_specs=[smem, smem, smem, vmem, vmem, vmem],
        out_specs=[vmem] * len(shapes),
        scratch_shapes=[pltpu.VMEM((cols, rows, LANES), jnp.float32)],
        name="pick",
    )(info, cnt, sel, sel, grad, res)


def keep_call(grad, res, sel, cnt, own_rows):
    rows, width = grad.shape
    cols = width // LANES
    shards, slots = sel.shape

    def kernel(cnt_s, sel_s, grad_v, res_v, out, acc):
        fill_blocks(grad_v, res_v, acc)
        zero = jnp.zeros((1, LANES), jnp.float32)

        def step(s, carry):
            used = cnt_s[s]
            for k in range(slots):
                b = sel_s[s, k]

                @pl.when(k < used)
                def _():
                    acc[b % cols, pl.ds(s * own_rows + b // cols, 1), :] = zero

            return carry

        lax.fori_loop(0, shards, step, 0)
        for c in range(cols):
            out[:, c * LANES : (c + 1) * LANES] = acc[c]

    smem = pl.BlockSpec(memory_space=pltpu.SMEM)
    vmem = pl.BlockSpec(memory_space=pltpu.VMEM)
    return pl.pallas_call(
        kernel,
        out_shape=jax.ShapeDtypeStruct((rows, width), jnp.float32),
        in_specs=[smem, smem, vmem, vmem],
        out_specs=vmem,
        scratch_shapes=[pltpu.VMEM((cols, rows, LANES), jnp.float32)],
        cost_estimate=pl.CostEstimate(flops=10**7, bytes_accessed=10**6, transcendentals=0),
        name="keep",
    )(cnt, sel, grad, res)


def merge_call(parts, slots, own_blocks):
    per = LANES // slots

    def kernel(*refs):
        out = refs[-1]
        views = []
        for ref in refs[:-1]:
            views += [ref] if len(ref.shape) == 2 else [ref.at[i] for i in range(ref.shape[0])]
        block = lax.broadcasted_iota(jnp.int32, (own_blocks, LANES), 0).astype(jnp.float32)
        total = jnp.zeros((own_blocks, LANES), jnp.float32)
        for at in range(0, len(views), per):
            group = views[at : at + per]
            ids = group[0][slots : slots + 1, :]
            for view in group[1:]:
                ids = jnp.maximum(ids, view[slots : slots + 1, :])
            x = [view[:slots, :] for view in group]
            x += [jnp.zeros((slots, LANES), jnp.float32)] * (per - len(group))
            x = jnp.concatenate(x, axis=0)
            hot = (block == ids).astype(jnp.float32).astype(jnp.bfloat16)
            high = x.astype(jnp.bfloat16)
            left = x - high.astype(jnp.float32)
            mid = left.astype(jnp.bfloat16)
            low = (left - mid.astype(jnp.float32)).astype(jnp.bfloat16)
            for piece in (high, mid, low):
                total = total + jnp.dot(hot, piece, preferred_element_type=jnp.float32)
        out[...] = total

    vmem = pl.BlockSpec(memory_space=pltpu.VMEM)
    return pl.pallas_call(
        kernel,
        out_shape=jax.ShapeDtypeStruct((own_blocks, LANES), jnp.float32),
        in_specs=[vmem] * len(parts),
        out_specs=vmem,
        name="merge",
    )(*parts)


def xor_send(x, axis, size, k):
    return lax.ppermute(x, axis, [(i, i ^ k) for i in range(size)])


def group_sum(x, groups):
    if not is_pow2(groups):
        return jnp.sum(lax.all_gather(x, "grp"), axis=0)
    bit = 1
    while bit < groups:
        wide = bit > 1 and bit * 2 < groups
        hops = (bit, 2 * bit, 3 * bit) if wide else (bit,)
        x = sum([xor_send(x, "grp", groups, k) for k in hops], x)
        bit *= 4 if wide else 2
    return x


def make_body(groups, shards):
    by_xor = is_pow2(shards) and shards <= 8

    def body(gradient, residual, selected, counts):
        rows, width = gradient.shape[2:]
        own_rows = rows // shards
        own_blocks = own_rows * width // LANES
        slots = selected.shape[3]
        grad, res, sel, cnt = gradient[0, 0], residual[0, 0], selected[0, 0], counts[0, 0]
        info = lax.axis_index("wide").astype(jnp.int32).reshape(1)
        packed = pick_call(grad, res, sel, cnt, info, shards, own_rows, by_xor)
        if by_xor:
            parts = [packed[0]] + [xor_send(packed[k], "wide", shards, k) for k in range(1, shards)]
        else:
            parts = [lax.all_to_all(packed[0], "wide", split_axis=0, concat_axis=0, tiled=True)]
        new_residual = keep_call(grad, res, sel, cnt, own_rows)[None, None]
        partial = merge_call(parts, slots, own_blocks)
        total = group_sum(partial, groups) / groups
        update = total.reshape(width // LANES, own_rows, LANES).transpose(1, 0, 2)
        return (update.reshape(1, own_rows, width), new_residual)

    return body


def solution(mesh):
    return jax.shard_map(
        make_body(mesh.shape["grp"], mesh.shape["wide"]),
        mesh=mesh,
        in_specs=(
            P("grp", "wide", None, None),
            P("grp", "wide", None, None),
            P("grp", "wide", None, None),
            P("grp", "wide", None),
        ),
        out_specs=(P("wide", None, None), P("grp", "wide", None, None)),
        check_vma=False,
    )
```

time: 92.1 us -> 27.3 us (0.30)
  waiting for transfers between devices: 59.3 us -> 7.96 us
  between operations: 14.1 us -> 0.65 us
  Pallas kernels: 0 us -> 7.13 us
  local copies, waits for them, and re-layouts: 3.13 us -> 0.61 us
  matrix products: 2.05 us -> 0 us
  other arithmetic: 2.93 us -> 1.5 us
  starting transfers between devices: 10.3 us -> 9.19 us
    psum x1 -> x0, waiting for transfers between devices: 52.4 us -> none  [body(): summed = lax.psum(partial_sum, 'grp')]
    all_to_all x2 -> x0, starting transfers between devices: 10.3 us -> none  [the longest x1 6.35 us: body(): lax.all_to_all(chosen_ids, 'wide', split_axis=0, concat_axis=0, tiled=True)]
    ppermute x0 -> x7, starting transfers between devices: none -> 9.19 us  [xor_send(): return lax.ppermute(x, axis, [(i, i ^ k) for i in range(size)])]
    ppermute x0 -> x7, waiting for transfers between devices: none -> 7.96 us  [xor_send(): return lax.ppermute(x, axis, [(i, i ^ k) for i in range(size)])]
    pallas_call x0 -> x3, Pallas kernels: none -> 7.13 us  [the longest x1 3.01 us: keep_call(): pl.pallas_call(kernel, out_shape=jax.ShapeDtypeStruct((rows, width), jnp....]
    all_to_all x2 -> x0, waiting for transfers between devices: 6.87 us -> none  [the longest x1 5.74 us: body(): lax.all_to_all(chosen, 'wide', split_axis=0, concat_axis=0, tiled=True)]
    dot_general x3 -> x0, matrix products: 2.05 us -> none  [the longest x1 0.95 us: body(): jnp.einsum('skb,skc->bc', arrived_hot, arrived, precision=lax.Precision.H...]
    unnamed x8 -> x6, local copies, waits for them, and re-layouts: 2.25 us -> 0.61 us
  transfers between devices with their start and end apart: 3 -> 7, of which waited for: 3 -> 5; matrix products, arithmetic and copies ran while one was open for 2% -> 0% of each run, Pallas kernels for 0% -> 11%
where the time goes in v1:
time: 27.3 us; the launch traced here: 27 us
  starting transfers between devices  9.19 us (34%)
  waiting for transfers between devices  7.96 us (29%)
  Pallas kernels  7.13 us (26%)
  other arithmetic  1.5 us (5%)
  between operations  0.65 us (2%)
  local copies, waits for them, and re-layouts  0.61 us (2%)
    ppermute x7, starting transfers between devices, xor_send(): return lax.ppermute(x, axis, [(i, i ^ k) for i in range(size)])  9.19 us
    ppermute x7, waiting for transfers between devices, xor_send(): return lax.ppermute(x, axis, [(i, i ^ k) for i in range(size)])  7.96 us
    pallas_call x1, Pallas kernels, keep_call(): pl.pallas_call(kernel, out_shape=jax.ShapeDtypeStruct((rows, width), jnp....  3.01 us
    pallas_call x1, Pallas kernels, pick_call(): pl.pallas_call(kernel, out_shape=shapes, in_specs=[smem, smem, smem, vmem...  2.53 us
    pallas_call x1, Pallas kernels, merge_call(): pl.pallas_call(kernel, out_shape=jax.ShapeDtypeStruct((own_blocks, LANES)...  1.58 us
    add x1, other arithmetic, group_sum(): x = sum([xor_send(x, 'grp', groups, k) for k in hops], x)  0.85 us
    div x1, other arithmetic, body(): total = group_sum(partial, groups) / groups  0.65 us
    unnamed x6, local copies, waits for them, and re-layouts  0.61 us
  transfers between devices with their start and end apart: 7, of which 5 were waited for; matrix products, arithmetic and copies ran while one was open for 0% of the time, Pallas kernels for 11%

profile of v1, /device:TPU:0, one launch (start us, length us, event | category | flops | bytes accessed | tf_op | source)
XLA Modules:
  0.0 27.0 jit_solution(6106023254514369477)
XLA Ops:
  0.6 2.5 %pick.1 = (f32[40,128]{1,0:T(8,128)}, f32[40,128]{1,0:T(8,128)}, f32[40,128]{1,0:T(8,128)}, f32[40,128]{1,0:T(8,128)}) custom-call(s32[1]{0:T(128)} %bitcast.info_s, s32[4]{0:T(128)} %bitcast.20, s32[4,32]{1,0:T(4,128)} %bitcast.17, s32[4,32]{1,0:T(4,128)} %bitcast.18, bf16[16,4096]{1,0:T(8,128)(2,1)} %bitcast.13, f32[16,4096]{1,0:T(8,128)} %bitcast.11), custom_call_target="tpu_custom_call" | custom-call | tf_op jit(solution)/shard_map/pick/pallas_call | solution.py:69
  3.2 3.1 %collective-permute-start = (f32[40,128]{1,0:T(8,128)}, f32[40,128]{1,0:T(8,128)S(1)}, u32[]{:S(2)}, u32[]{:S(2)}) collective-permute-start(f32[40,128]{1,0:T(8,128)} %get-tuple-element.7), channel_id=1, source_target_pairs={{0,1},{1,0},{2,3},{3,2},{4,5},{5,4},{6,7},{7,6},{8,9},{9,8},{10,11... | collective-permute-start | bytes 61448 | tf_op jit(solution)/shard_map/ppermute | solution.py:154
  6.2 2.6 %collective-permute-start.1 = (f32[40,128]{1,0:T(8,128)}, f32[40,128]{1,0:T(8,128)S(1)}, u32[]{:S(2)}, u32[]{:S(2)}) collective-permute-start(f32[40,128]{1,0:T(8,128)} %get-tuple-element.8), channel_id=1, source_target_pairs={{0,2},{1,3},{2,0},{3,1},{4,6},{5,7},{6,4},{7,5},{8,10},{9,11},{10,... | collective-permute-start | bytes 61448 | tf_op jit(solution)/shard_map/ppermute | solution.py:154
  8.8 0.0 collective-permute-start.2
  8.8 0.0 collective-permute-done.refs_1_
  8.8 0.0 copy-start
  8.8 2.5 %collective-permute-done.1.refs_2_ = f32[40,128]{1,0:T(8,128)S(1)} collective-permute-done((f32[40,128]{1,0:T(8,128)}, f32[40,128]{1,0:T(8,128)S(1)}, u32[]{:S(2)}, u32[]{:S(2)}) %collective-permute-start.1) | collective-permute-done | bytes 20512 | tf_op jit(solution)/shard_map/ppermute | solution.py:154
  11.3 0.0 copy-start.1
  11.3 3.3 %collective-permute-done.2.refs_3_ = f32[40,128]{1,0:T(8,128)S(1)} collective-permute-done((f32[40,128]{1,0:T(8,128)}, f32[40,128]{1,0:T(8,128)S(1)}, u32[]{:S(2)}, u32[]{:S(2)}) %collective-permute-start.2) | collective-permute-done | bytes 20512 | tf_op jit(solution)/shard_map/ppermute | solution.py:154
  14.6 0.0 copy-start.2
  14.6 0.0 copy-done
  14.6 0.0 copy-done.1
  14.6 0.6 %copy-done.2 = f32[40,128]{1,0:T(8,128)} copy-done((f32[40,128]{1,0:T(8,128)}, f32[40,128]{1,0:T(8,128)S(1)}, u32[]{:S(2)}) %copy-start.2) | copy-done | bytes 20504
  15.2 1.6 %merge.1 = f32[128,128]{1,0:T(8,128)} custom-call(f32[40,128]{1,0:T(8,128)} %get-tuple-element.6.refs_0_, f32[40,128]{1,0:T(8,128)} %copy-done, f32[40,128]{1,0:T(8,128)} %copy-done.1, f32[40,128]{1,0:T(8,128)} %copy-done.2), custom_call_target="tpu_custom_call" | custom-call | tf_op jit(solution)/shard_map/merge/pallas_call | solution.py:144
  16.8 0.0 collective-permute-start.3
  16.8 1.5 %collective-permute-done.3 = f32[128,128]{1,0:T(8,128)S(1)} collective-permute-done((f32[128,128]{1,0:T(8,128)}, f32[128,128]{1,0:T(8,128)S(1)}, u32[]{:S(2)}, u32[]{:S(2)}) %collective-permute-start.3) | collective-permute-done | bytes 65568 | tf_op jit(solution)/shard_map/ppermute | solution.py:154
  18.3 0.9 %add.12 = f32[128,128]{1,0:T(8,128)S(1)} add(f32[128,128]{1,0:T(8,128)} %merge.1, f32[128,128]{1,0:T(8,128)S(1)} %collective-permute-done.3) | non-fusion elementwise | flops 16384 | bytes 196608 | tf_op jit(solution)/shard_map/add | solution.py:164
  19.1 2.5 %collective-permute-start.6 = (f32[128,128]{1,0:T(8,128)S(1)}, f32[128,128]{1,0:T(8,128)S(1)}, u32[]{:S(2)}, u32[]{:S(2)}) collective-permute-start(f32[128,128]{1,0:T(8,128)S(1)} %add.12), channel_id=1, source_target_pairs={{0,24},{4,28},{8,16},{12,20},{16,8},{20,12},{24,0},{28,4},{1,25},{... | collective-permute-start | bytes 196616 | tf_op jit(solution)/shard_map/ppermute | solution.py:154
  21.6 0.5 %collective-permute-start.5 = (f32[128,128]{1,0:T(8,128)S(1)}, f32[128,128]{1,0:T(8,128)S(1)}, u32[]{:S(2)}, u32[]{:S(2)}) collective-permute-start(f32[128,128]{1,0:T(8,128)S(1)} %add.12), channel_id=1, source_target_pairs={{0,16},{4,20},{8,24},{12,28},{16,0},{20,4},{24,8},{28,12},{1,17},{... | collective-permute-start | bytes 196616 | tf_op jit(solution)/shard_map/ppermute | solution.py:154
  22.1 0.5 %collective-permute-start.4 = (f32[128,128]{1,0:T(8,128)S(1)}, f32[128,128]{1,0:T(8,128)S(1)}, u32[]{:S(2)}, u32[]{:S(2)}) collective-permute-start(f32[128,128]{1,0:T(8,128)S(1)} %add.12), channel_id=1, source_target_pairs={{0,8},{4,12},{8,0},{12,4},{16,24},{20,28},{24,16},{28,20},{1,9},{5... | collective-permute-start | bytes 196616 | tf_op jit(solution)/shard_map/ppermute | solution.py:154
  22.7 3.0 %keep.1 = f32[16,4096]{1,0:T(8,128)} custom-call(s32[4]{0:T(128)} %bitcast.21, s32[4,32]{1,0:T(4,128)} %bitcast.19, bf16[16,4096]{1,0:T(8,128)(2,1)} %bitcast.14, f32[16,4096]{1,0:T(8,128)} %bitcast.12), custom_call_target="tpu_custom_call" | custom-call | flops 10000000 | bytes 1000000 | tf_op jit(solution)/shard_map/keep/pallas_call | solution.py:105
  25.7 0.0 collective-permute-done.6
  25.7 0.2 collective-permute-done.5
  25.9 0.5 %collective-permute-done.4 = f32[128,128]{1,0:T(8,128)S(1)} collective-permute-done((f32[128,128]{1,0:T(8,128)S(1)}, f32[128,128]{1,0:T(8,128)S(1)}, u32[]{:S(2)}, u32[]{:S(2)}) %collective-permute-start.4) | collective-permute-done | bytes 65568 | tf_op jit(solution)/shard_map/ppermute | solution.py:154
  26.4 0.6 %add_multiply_fusion = f32[128,128]{1,0:T(8,128)} fusion(f32[128,128]{1,0:T(8,128)S(1)} %collective-permute-done.6, f32[128,128]{1,0:T(8,128)S(1)} %collective-permute-done.5, f32[128,128]{1,0:T(8,128)S(1)} %add.12, f32[128,128]{1,0:T(8,128)S(1)} %collective-permute-done.4), kind=kLoop, calls=%fused_computation | loop fusion | flops 65536 | bytes 327680 | tf_op jit(solution)/shard_map/div | solution.py:186
Async XLA Ops:
  3.2 5.6 %collective-permute-start = (f32[40,128]{1,0:T(8,128)}, f32[40,128]{1,0:T(8,128)S(1)}, u32[]{:S(2)}, u32[]{:S(2)}) collective-permute-start(f32[40,128]{1,0:T(8,128)} %get-tuple-element.7), channel_id=1, source_target_pairs={{0,1},{1,0},{2,3},{3,2},{4,5},{5,4},{6,7},{7,6},{8,9},{9,8},{10,11... | collective-permute-start | bytes 61448 | tf_op jit(solution)/shard_map/ppermute | solution.py:154
  6.2 5.1 %collective-permute-start.1 = (f32[40,128]{1,0:T(8,128)}, f32[40,128]{1,0:T(8,128)S(1)}, u32[]{:S(2)}, u32[]{:S(2)}) collective-permute-start(f32[40,128]{1,0:T(8,128)} %get-tuple-element.8), channel_id=1, source_target_pairs={{0,2},{1,3},{2,0},{3,1},{4,6},{5,7},{6,4},{7,5},{8,10},{9,11},{10,... | collective-permute-start | bytes 61448 | tf_op jit(solution)/shard_map/ppermute | solution.py:154
  8.8 5.8 %collective-permute-start.2 = (f32[40,128]{1,0:T(8,128)}, f32[40,128]{1,0:T(8,128)S(1)}, u32[]{:S(2)}, u32[]{:S(2)}) collective-permute-start(f32[40,128]{1,0:T(8,128)} %get-tuple-element.9), channel_id=1, source_target_pairs={{0,3},{1,2},{2,1},{3,0},{4,7},{5,6},{6,5},{7,4},{8,11},{9,10},{10,... | collective-permute-start | bytes 61448 | tf_op jit(solution)/shard_map/ppermute | solution.py:154
  8.8 5.8 %copy-start = (f32[40,128]{1,0:T(8,128)}, f32[40,128]{1,0:T(8,128)S(1)}, u32[]{:S(2)}) copy-start(f32[40,128]{1,0:T(8,128)S(1)} %collective-permute-done.refs_1_) | copy-start | bytes 61444
  11.3 3.3 %copy-start.1 = (f32[40,128]{1,0:T(8,128)}, f32[40,128]{1,0:T(8,128)S(1)}, u32[]{:S(2)}) copy-start(f32[40,128]{1,0:T(8,128)S(1)} %collective-permute-done.1.refs_2_) | copy-start | bytes 61444
  14.6 0.6 %copy-start.2 = (f32[40,128]{1,0:T(8,128)}, f32[40,128]{1,0:T(8,128)S(1)}, u32[]{:S(2)}) copy-start(f32[40,128]{1,0:T(8,128)S(1)} %collective-permute-done.2.refs_3_) | copy-start | bytes 61444
  16.8 1.5 %collective-permute-start.3 = (f32[128,128]{1,0:T(8,128)}, f32[128,128]{1,0:T(8,128)S(1)}, u32[]{:S(2)}, u32[]{:S(2)}) collective-permute-start(f32[128,128]{1,0:T(8,128)} %merge.1), channel_id=1, source_target_pairs={{0,4},{4,0},{8,12},{12,8},{16,20},{20,16},{24,28},{28,24},{1,5},{5... | collective-permute-start | bytes 196616 | tf_op jit(solution)/shard_map/ppermute | solution.py:154
  19.1 6.6 %collective-permute-start.6 = (f32[128,128]{1,0:T(8,128)S(1)}, f32[128,128]{1,0:T(8,128)S(1)}, u32[]{:S(2)}, u32[]{:S(2)}) collective-permute-start(f32[128,128]{1,0:T(8,128)S(1)} %add.12), channel_id=1, source_target_pairs={{0,24},{4,28},{8,16},{12,20},{16,8},{20,12},{24,0},{28,4},{1,25},{... | collective-permute-start | bytes 196616 | tf_op jit(solution)/shard_map/ppermute | solution.py:154
  21.6 4.3 %collective-permute-start.5 = (f32[128,128]{1,0:T(8,128)S(1)}, f32[128,128]{1,0:T(8,128)S(1)}, u32[]{:S(2)}, u32[]{:S(2)}) collective-permute-start(f32[128,128]{1,0:T(8,128)S(1)} %add.12), channel_id=1, source_target_pairs={{0,16},{4,20},{8,24},{12,28},{16,0},{20,4},{24,8},{28,12},{1,17},{... | collective-permute-start | bytes 196616 | tf_op jit(solution)/shard_map/ppermute | solution.py:154
  22.1 4.3 %collective-permute-start.4 = (f32[128,128]{1,0:T(8,128)S(1)}, f32[128,128]{1,0:T(8,128)S(1)}, u32[]{:S(2)}, u32[]{:S(2)}) collective-permute-start(f32[128,128]{1,0:T(8,128)S(1)} %add.12), channel_id=1, source_target_pairs={{0,8},{4,12},{8,0},{12,4},{16,24},{20,28},{24,16},{28,20},{1,9},{5... | collective-permute-start | bytes 196616 | tf_op jit(solution)/shard_map/ppermute | solution.py:154

commit v2 on v1

--- a/solution.py
+++ b/solution.py
@@ -63,7 +63,7 @@
     smem = pl.BlockSpec(memory_space=pltpu.SMEM)
     vmem = pl.BlockSpec(memory_space=pltpu.VMEM)
     size = (slots + PAD, LANES)
-    shapes = [jax.ShapeDtypeStruct(size, jnp.float32)] * shards
+    shapes = [pltpu.VMEM(size, jnp.float32)] * shards
     if not by_xor:
         shapes = [jax.ShapeDtypeStruct((shards,) + size, jnp.float32)]
     return pl.pallas_call(
@@ -113,7 +113,7 @@
     )(cnt, sel, grad, res)
 
 
-def merge_call(parts, slots, own_blocks):
+def merge_call(parts, slots, own_blocks, chunk):
     per = LANES // slots
 
     def kernel(*refs):
@@ -123,8 +123,8 @@
             views += [ref] if len(ref.shape) == 2 else [ref.at[i] for i in range(ref.shape[0])]
         block = lax.broadcasted_iota(jnp.int32, (own_blocks, LANES), 0).astype(jnp.float32)
         total = jnp.zeros((own_blocks, LANES), jnp.float32)
-        for at in range(0, len(views), per):
-            group = views[at : at + per]
+        for at in range(0, len(views), chunk):
+            group = views[at : at + chunk]
             ids = group[0][slots : slots + 1, :]
             for view in group[1:]:
                 ids = jnp.maximum(ids, view[slots : slots + 1, :])
@@ -143,21 +143,20 @@
     vmem = pl.BlockSpec(memory_space=pltpu.VMEM)
     return pl.pallas_call(
         kernel,
-        out_shape=jax.ShapeDtypeStruct((own_blocks, LANES), jnp.float32),
+        out_shape=pltpu.VMEM((own_blocks, LANES), jnp.float32),
         in_specs=[vmem] * len(parts),
         out_specs=vmem,
         name="merge",
-    )(*parts)
+    )(*[pltpu.with_memory_space_constraint(p, pltpu.VMEM) for p in parts])
 
 
 def xor_send(x, axis, size, k):
     return lax.ppermute(x, axis, [(i, i ^ k) for i in range(size)])
 
 
-def group_sum(x, groups):
+def group_sum(x, groups, bit):
     if not is_pow2(groups):
         return jnp.sum(lax.all_gather(x, "grp"), axis=0)
-    bit = 1
     while bit < groups:
         wide = bit > 1 and bit * 2 < groups
         hops = (bit, 2 * bit, 3 * bit) if wide else (bit,)
@@ -168,6 +167,7 @@
 
 def make_body(groups, shards):
     by_xor = is_pow2(shards) and shards <= 8
+    early = by_xor and is_pow2(groups) and groups > 1
 
     def body(gradient, residual, selected, counts):
         rows, width = gradient.shape[2:]
@@ -178,12 +178,16 @@
         info = lax.axis_index("wide").astype(jnp.int32).reshape(1)
         packed = pick_call(grad, res, sel, cnt, info, shards, own_rows, by_xor)
         if by_xor:
-            parts = [packed[0]] + [xor_send(packed[k], "wide", shards, k) for k in range(1, shards)]
+            parts = [xor_send(packed[k], "wide", shards, k) for k in reversed(range(1, shards))]
+            parts = [packed[0]] + parts[::-1]
+            if early:
+                parts += [xor_send(part, "grp", groups, 1) for part in parts]
         else:
             parts = [lax.all_to_all(packed[0], "wide", split_axis=0, concat_axis=0, tiled=True)]
         new_residual = keep_call(grad, res, sel, cnt, own_rows)[None, None]
-        partial = merge_call(parts, slots, own_blocks)
-        total = group_sum(partial, groups) / groups
+        chunk = min(LANES // slots, shards)
+        partial = merge_call(parts, slots, own_blocks, chunk)
+        total = group_sum(partial, groups, 2 if early else 1) / groups
         update = total.reshape(width // LANES, own_rows, LANES).transpose(1, 0, 2)
         return (update.reshape(1, own_rows, width), new_residual)
 

time: 27.3 us -> 23.3 us (0.85)
  Pallas kernels: 7.13 us -> 5.16 us
  waiting for transfers between devices: 7.96 us -> 6.92 us
  other arithmetic: 1.5 us -> 0.65 us
  local copies, waits for them, and re-layouts: 0.61 us -> 0 us
  starting transfers between devices: 9.19 us -> 9.78 us
    pallas_call x1, Pallas kernels: 1.58 us -> 0.2 us  [merge_call(): pl.pallas_call(kernel, out_shape=pltpu.VMEM((own_blocks, LANES), jnp.floa...]
    ppermute x7 -> x10, waiting for transfers between devices: 7.96 us -> 6.92 us  [xor_send(): return lax.ppermute(x, axis, [(i, i ^ k) for i in range(size)])]
    add x1 -> x0, other arithmetic: 0.85 us -> none  [group_sum(): x = sum([xor_send(x, 'grp', groups, k) for k in hops], x)]
    pallas_call x1, Pallas kernels: 2.53 us -> 1.91 us  [pick_call(): pl.pallas_call(kernel, out_shape=shapes, in_specs=[smem, smem, smem, vmem...]
    unnamed x6 -> x0, local copies, waits for them, and re-layouts: 0.61 us -> none
    ppermute x7 -> x10, starting transfers between devices: 9.19 us -> 9.78 us  [xor_send(): return lax.ppermute(x, axis, [(i, i ^ k) for i in range(size)])]
  transfers between devices with their start and end apart: 7 -> 10, of which waited for: 5 -> 5; matrix products, arithmetic and copies ran while one was open for 0% -> 0% of each run, Pallas kernels for 11% -> 13%
where the time goes in v2:
time: 23.3 us; the launch traced here: 23.2 us
  starting transfers between devices  9.78 us (42%)
  waiting for transfers between devices  6.92 us (30%)
  Pallas kernels  5.16 us (22%)
  between operations  0.67 us (3%)
  other arithmetic  0.65 us (3%)
    ppermute x10, starting transfers between devices, xor_send(): return lax.ppermute(x, axis, [(i, i ^ k) for i in range(size)])  9.78 us
    ppermute x10, waiting for transfers between devices, xor_send(): return lax.ppermute(x, axis, [(i, i ^ k) for i in range(size)])  6.92 us
    pallas_call x1, Pallas kernels, keep_call(): pl.pallas_call(kernel, out_shape=jax.ShapeDtypeStruct((rows, width), jnp....  3.04 us
    pallas_call x1, Pallas kernels, pick_call(): pl.pallas_call(kernel, out_shape=shapes, in_specs=[smem, smem, smem, vmem...  1.91 us
    div x1, other arithmetic, body(): total = group_sum(partial, groups, 2 if early else 1) / groups  0.65 us
  transfers between devices with their start and end apart: 10, of which 5 were waited for; matrix products, arithmetic and copies ran while one was open for 0% of the time, Pallas kernels for 13%

profile of v2, /device:TPU:0, one launch (start us, length us, event | category | flops | bytes accessed | tf_op | source)
XLA Modules:
  0.0 23.2 jit_solution(16450892478827228897)
XLA Ops:
  0.6 1.9 %pick.1 = (f32[40,128]{1,0:T(8,128)S(1)}, f32[40,128]{1,0:T(8,128)S(1)}, f32[40,128]{1,0:T(8,128)S(1)}, f32[40,128]{1,0:T(8,128)S(1)}) custom-call(s32[1]{0:T(128)} %bitcast.info_s, s32[4]{0:T(128)} %bitcast.20, s32[4,32]{1,0:T(4,128)} %bitcast.17, s32[4,32]{1,0:T(4,128)} %bitcast.18, bf16[16,4096]{1,0:T(8,128)(2,1)} %bitcast.13, f32[16,4096]{1,0:T(8,128)} %bitcast.11), custom_call_target="tpu_custom_call" | custom-call | tf_op jit(solution)/shard_map/pick/pallas_call | solution.py:69
  2.6 3.1 %collective-permute-start = (f32[40,128]{1,0:T(8,128)S(1)}, f32[40,128]{1,0:T(8,128)S(1)}, u32[]{:S(2)}, u32[]{:S(2)}) collective-permute-start(f32[40,128]{1,0:T(8,128)S(1)} %get-tuple-element.7), channel_id=1, source_target_pairs={{0,1},{1,0},{2,3},{3,2},{4,5},{5,4},{6,7},{7,6},{8,9},{9,8},{10,11... | collective-permute-start | bytes 61448 | tf_op jit(solution)/shard_map/ppermute | solution.py:154
  5.7 2.6 %collective-permute-start.1 = (f32[40,128]{1,0:T(8,128)S(1)}, f32[40,128]{1,0:T(8,128)S(1)}, u32[]{:S(2)}, u32[]{:S(2)}) collective-permute-start(f32[40,128]{1,0:T(8,128)S(1)} %get-tuple-element.8), channel_id=1, source_target_pairs={{0,2},{1,3},{2,0},{3,1},{4,6},{5,7},{6,4},{7,5},{8,10},{9,11},{10,... | collective-permute-start | bytes 61448 | tf_op jit(solution)/shard_map/ppermute | solution.py:154
  8.3 0.0 collective-permute-start.2
  8.3 0.0 collective-permute-start.3
  8.3 0.0 collective-permute-done.refs_1_
  8.3 0.5 %collective-permute-start.4 = (f32[40,128]{1,0:T(8,128)S(1)}, f32[40,128]{1,0:T(8,128)S(1)}, u32[]{:S(2)}, u32[]{:S(2)}) collective-permute-start(f32[40,128]{1,0:T(8,128)S(1)} %collective-permute-done.refs_1_), channel_id=1, source_target_pairs={{0,4},{4,0},{8,12},{12,8},{16,20},{20,16},{24,28},{28,24},{1,5},{5... | collective-permute-start | bytes 61448 | tf_op jit(solution)/shard_map/ppermute | solution.py:154
  8.8 1.8 %collective-permute-done.1.refs_2_ = f32[40,128]{1,0:T(8,128)S(1)} collective-permute-done((f32[40,128]{1,0:T(8,128)S(1)}, f32[40,128]{1,0:T(8,128)S(1)}, u32[]{:S(2)}, u32[]{:S(2)}) %collective-permute-start.1) | collective-permute-done | bytes 20512 | tf_op jit(solution)/shard_map/ppermute | solution.py:154
  10.6 0.0 collective-permute-start.5
  10.6 3.3 %collective-permute-done.2.refs_3_ = f32[40,128]{1,0:T(8,128)S(1)} collective-permute-done((f32[40,128]{1,0:T(8,128)S(1)}, f32[40,128]{1,0:T(8,128)S(1)}, u32[]{:S(2)}, u32[]{:S(2)}) %collective-permute-start.2) | collective-permute-done | bytes 20512 | tf_op jit(solution)/shard_map/ppermute | solution.py:154
  13.8 0.0 collective-permute-start.6
  13.8 0.0 collective-permute-done.3.refs_4_
  13.8 0.0 collective-permute-done.4.refs_5_
  13.9 0.0 collective-permute-done.5.refs_6_
  13.9 1.2 %collective-permute-done.6.refs_7_ = f32[40,128]{1,0:T(8,128)S(1)} collective-permute-done((f32[40,128]{1,0:T(8,128)S(1)}, f32[40,128]{1,0:T(8,128)S(1)}, u32[]{:S(2)}, u32[]{:S(2)}) %collective-permute-start.6) | collective-permute-done | bytes 20512 | tf_op jit(solution)/shard_map/ppermute | solution.py:154
  15.0 0.2 merge.1
  15.2 2.5 %collective-permute-start.9 = (f32[128,128]{1,0:T(8,128)S(1)}, f32[128,128]{1,0:T(8,128)S(1)}, u32[]{:S(2)}, u32[]{:S(2)}) collective-permute-start(f32[128,128]{1,0:T(8,128)S(1)} %merge.1), channel_id=1, source_target_pairs={{0,24},{4,28},{8,16},{12,20},{16,8},{20,12},{24,0},{28,4},{1,25},{... | collective-permute-start | bytes 196616 | tf_op jit(solution)/shard_map/ppermute | solution.py:154
  17.8 0.5 %collective-permute-start.8 = (f32[128,128]{1,0:T(8,128)S(1)}, f32[128,128]{1,0:T(8,128)S(1)}, u32[]{:S(2)}, u32[]{:S(2)}) collective-permute-start(f32[128,128]{1,0:T(8,128)S(1)} %merge.1), channel_id=1, source_target_pairs={{0,16},{4,20},{8,24},{12,28},{16,0},{20,4},{24,8},{28,12},{1,17},{... | collective-permute-start | bytes 196616 | tf_op jit(solution)/shard_map/ppermute | solution.py:154
  18.3 0.5 %collective-permute-start.7 = (f32[128,128]{1,0:T(8,128)S(1)}, f32[128,128]{1,0:T(8,128)S(1)}, u32[]{:S(2)}, u32[]{:S(2)}) collective-permute-start(f32[128,128]{1,0:T(8,128)S(1)} %merge.1), channel_id=1, source_target_pairs={{0,8},{4,12},{8,0},{12,4},{16,24},{20,28},{24,16},{28,20},{1,9},{5... | collective-permute-start | bytes 196616 | tf_op jit(solution)/shard_map/ppermute | solution.py:154
  18.8 3.0 %keep.1 = f32[16,4096]{1,0:T(8,128)} custom-call(s32[4]{0:T(128)} %bitcast.21, s32[4,32]{1,0:T(4,128)} %bitcast.19, bf16[16,4096]{1,0:T(8,128)(2,1)} %bitcast.14, f32[16,4096]{1,0:T(8,128)} %bitcast.12), custom_call_target="tpu_custom_call" | custom-call | flops 10000000 | bytes 1000000 | tf_op jit(solution)/shard_map/keep/pallas_call | solution.py:105
  21.8 0.0 collective-permute-done.9
  21.8 0.2 collective-permute-done.8
  22.0 0.5 %collective-permute-done.7 = f32[128,128]{1,0:T(8,128)S(1)} collective-permute-done((f32[128,128]{1,0:T(8,128)S(1)}, f32[128,128]{1,0:T(8,128)S(1)}, u32[]{:S(2)}, u32[]{:S(2)}) %collective-permute-start.7) | collective-permute-done | bytes 65568 | tf_op jit(solution)/shard_map/ppermute | solution.py:154
  22.5 0.6 %add_multiply_fusion = f32[128,128]{1,0:T(8,128)} fusion(f32[128,128]{1,0:T(8,128)S(1)} %collective-permute-done.9, f32[128,128]{1,0:T(8,128)S(1)} %collective-permute-done.8, f32[128,128]{1,0:T(8,128)S(1)} %merge.1, f32[128,128]{1,0:T(8,128)S(1)} %collective-permute-done.7), kind=kLoop, calls=%fused_computation | loop fusion | flops 65536 | bytes 327680 | tf_op jit(solution)/shard_map/div | solution.py:190
Async XLA Ops:
  2.6 5.7 %collective-permute-start = (f32[40,128]{1,0:T(8,128)S(1)}, f32[40,128]{1,0:T(8,128)S(1)}, u32[]{:S(2)}, u32[]{:S(2)}) collective-permute-start(f32[40,128]{1,0:T(8,128)S(1)} %get-tuple-element.7), channel_id=1, source_target_pairs={{0,1},{1,0},{2,3},{3,2},{4,5},{5,4},{6,7},{7,6},{8,9},{9,8},{10,11... | collective-permute-start | bytes 61448 | tf_op jit(solution)/shard_map/ppermute | solution.py:154
  5.7 4.9 %collective-permute-start.1 = (f32[40,128]{1,0:T(8,128)S(1)}, f32[40,128]{1,0:T(8,128)S(1)}, u32[]{:S(2)}, u32[]{:S(2)}) collective-permute-start(f32[40,128]{1,0:T(8,128)S(1)} %get-tuple-element.8), channel_id=1, source_target_pairs={{0,2},{1,3},{2,0},{3,1},{4,6},{5,7},{6,4},{7,5},{8,10},{9,11},{10,... | collective-permute-start | bytes 61448 | tf_op jit(solution)/shard_map/ppermute | solution.py:154
  8.3 5.6 %collective-permute-start.2 = (f32[40,128]{1,0:T(8,128)S(1)}, f32[40,128]{1,0:T(8,128)S(1)}, u32[]{:S(2)}, u32[]{:S(2)}) collective-permute-start(f32[40,128]{1,0:T(8,128)S(1)} %get-tuple-element.9), channel_id=1, source_target_pairs={{0,3},{1,2},{2,1},{3,0},{4,7},{5,6},{6,5},{7,4},{8,11},{9,10},{10,... | collective-permute-start | bytes 61448 | tf_op jit(solution)/shard_map/ppermute | solution.py:154
  8.3 5.6 %collective-permute-start.3 = (f32[40,128]{1,0:T(8,128)S(1)}, f32[40,128]{1,0:T(8,128)S(1)}, u32[]{:S(2)}, u32[]{:S(2)}) collective-permute-start(f32[40,128]{1,0:T(8,128)S(1)} %get-tuple-element.6.refs_0_), channel_id=1, source_target_pairs={{0,4},{4,0},{8,12},{12,8},{16,20},{20,16},{24,28},{28,24},{1,5},{5... | collective-permute-start | bytes 61448 | tf_op jit(solution)/shard_map/ppermute | solution.py:154
  8.3 5.6 %collective-permute-start.4 = (f32[40,128]{1,0:T(8,128)S(1)}, f32[40,128]{1,0:T(8,128)S(1)}, u32[]{:S(2)}, u32[]{:S(2)}) collective-permute-start(f32[40,128]{1,0:T(8,128)S(1)} %collective-permute-done.refs_1_), channel_id=1, source_target_pairs={{0,4},{4,0},{8,12},{12,8},{16,20},{20,16},{24,28},{28,24},{1,5},{5... | collective-permute-start | bytes 61448 | tf_op jit(solution)/shard_map/ppermute | solution.py:154
  10.6 3.3 %collective-permute-start.5 = (f32[40,128]{1,0:T(8,128)S(1)}, f32[40,128]{1,0:T(8,128)S(1)}, u32[]{:S(2)}, u32[]{:S(2)}) collective-permute-start(f32[40,128]{1,0:T(8,128)S(1)} %collective-permute-done.1.refs_2_), channel_id=1, source_target_pairs={{0,4},{4,0},{8,12},{12,8},{16,20},{20,16},{24,28},{28,24},{1,5},{5... | collective-permute-start | bytes 61448 | tf_op jit(solution)/shard_map/ppermute | solution.py:154
  13.8 1.2 %collective-permute-start.6 = (f32[40,128]{1,0:T(8,128)S(1)}, f32[40,128]{1,0:T(8,128)S(1)}, u32[]{:S(2)}, u32[]{:S(2)}) collective-permute-start(f32[40,128]{1,0:T(8,128)S(1)} %collective-permute-done.2.refs_3_), channel_id=1, source_target_pairs={{0,4},{4,0},{8,12},{12,8},{16,20},{20,16},{24,28},{28,24},{1,5},{5... | collective-permute-start | bytes 61448 | tf_op jit(solution)/shard_map/ppermute | solution.py:154
  15.2 6.6 %collective-permute-start.9 = (f32[128,128]{1,0:T(8,128)S(1)}, f32[128,128]{1,0:T(8,128)S(1)}, u32[]{:S(2)}, u32[]{:S(2)}) collective-permute-start(f32[128,128]{1,0:T(8,128)S(1)} %merge.1), channel_id=1, source_target_pairs={{0,24},{4,28},{8,16},{12,20},{16,8},{20,12},{24,0},{28,4},{1,25},{... | collective-permute-start | bytes 196616 | tf_op jit(solution)/shard_map/ppermute | solution.py:154
  17.8 4.3 %collective-permute-start.8 = (f32[128,128]{1,0:T(8,128)S(1)}, f32[128,128]{1,0:T(8,128)S(1)}, u32[]{:S(2)}, u32[]{:S(2)}) collective-permute-start(f32[128,128]{1,0:T(8,128)S(1)} %merge.1), channel_id=1, source_target_pairs={{0,16},{4,20},{8,24},{12,28},{16,0},{20,4},{24,8},{28,12},{1,17},{... | collective-permute-start | bytes 196616 | tf_op jit(solution)/shard_map/ppermute | solution.py:154
  18.3 4.3 %collective-permute-start.7 = (f32[128,128]{1,0:T(8,128)S(1)}, f32[128,128]{1,0:T(8,128)S(1)}, u32[]{:S(2)}, u32[]{:S(2)}) collective-permute-start(f32[128,128]{1,0:T(8,128)S(1)} %merge.1), channel_id=1, source_target_pairs={{0,8},{4,12},{8,0},{12,4},{16,24},{20,28},{24,16},{28,20},{1,9},{5... | collective-permute-start | bytes 196616 | tf_op jit(solution)/shard_map/ppermute | solution.py:154

commit v3 on v2

--- a/solution.py
+++ b/solution.py
@@ -5,12 +5,19 @@
 from jax.experimental.pallas import tpu as pltpu
 from jax.sharding import PartitionSpec as P
 
+
 LANES = 128
 PAD = 8
 
 
 def is_pow2(n):
     return n & (n - 1) == 0
+
+
+def row_and_col(b, cols):
+    if is_pow2(cols):
+        return b >> (cols.bit_length() - 1), b & (cols - 1)
+    return b // cols, b % cols
 
 
 def fill_blocks(grad, res, acc):
@@ -33,11 +40,11 @@
 
         def pack(shard, off, put):
             for k in range(slots):
-                b = sel_s[shard, k]
-                row = shard * own_rows + b // cols
-                put(k, 1, acc[b % cols, pl.ds(row, 1), :])
+                row, col = row_and_col(sel_s[shard, k], cols)
+                put(k, 1, acc[col, pl.ds(shard * own_rows + row, 1), :])
             ids = sel_v[pl.ds(shard, 1), :]
-            ids = (ids % cols) * own_rows + ids // cols
+            row, col = row_and_col(ids, cols)
+            ids = col * own_rows + row
             ids = jnp.concatenate([ids] * per, axis=1)
             keep = (lane // slots == off) & (lane % slots < cnt_s[shard])
             ids = jnp.where(keep, ids, -1).astype(jnp.float32)
@@ -88,11 +95,11 @@
         def step(s, carry):
             used = cnt_s[s]
             for k in range(slots):
-                b = sel_s[s, k]
+                row, col = row_and_col(sel_s[s, k], cols)
 
                 @pl.when(k < used)
                 def _():
-                    acc[b % cols, pl.ds(s * own_rows + b // cols, 1), :] = zero
+                    acc[col, pl.ds(s * own_rows + row, 1), :] = zero
 
             return carry
 

time: 23.3 us -> 22.8 us (0.979)
  Pallas kernels: 5.16 us -> 4.15 us
  waiting for transfers between devices: 6.92 us -> 7.36 us
    pallas_call x1, Pallas kernels: 1.91 us -> 1.34 us  [pick_call(): pl.pallas_call(kernel, out_shape=shapes, in_specs=[smem, smem, smem, vmem...]
    ppermute x10, waiting for transfers between devices: 6.92 us -> 7.36 us  [xor_send(): return lax.ppermute(x, axis, [(i, i ^ k) for i in range(size)])]
    pallas_call x1, Pallas kernels: 3.04 us -> 2.61 us  [keep_call(): pl.pallas_call(kernel, out_shape=jax.ShapeDtypeStruct((rows, width), jnp....]
  transfers between devices with their start and end apart: 10 -> 10, of which waited for: 5 -> 5; matrix products, arithmetic and copies ran while one was open for 0% -> 0% of each run, Pallas kernels for 13% -> 12%
where the time goes in v3:
time: 22.8 us; the launch traced here: 22.6 us
  starting transfers between devices  9.78 us (43%)
  waiting for transfers between devices  7.36 us (32%)
  Pallas kernels  4.15 us (18%)
  between operations  0.67 us (3%)
  other arithmetic  0.65 us (3%)
    ppermute x10, starting transfers between devices, xor_send(): return lax.ppermute(x, axis, [(i, i ^ k) for i in range(size)])  9.78 us
    ppermute x10, waiting for transfers between devices, xor_send(): return lax.ppermute(x, axis, [(i, i ^ k) for i in range(size)])  7.36 us
    pallas_call x1, Pallas kernels, keep_call(): pl.pallas_call(kernel, out_shape=jax.ShapeDtypeStruct((rows, width), jnp....  2.61 us
    pallas_call x1, Pallas kernels, pick_call(): pl.pallas_call(kernel, out_shape=shapes, in_specs=[smem, smem, smem, vmem...  1.34 us
    div x1, other arithmetic, body(): total = group_sum(partial, groups, 2 if early else 1) / groups  0.65 us
  transfers between devices with their start and end apart: 10, of which 5 were waited for; matrix products, arithmetic and copies ran while one was open for 0% of the time, Pallas kernels for 12%

profile of v3, /device:TPU:0, one launch (start us, length us, event | category | flops | bytes accessed | tf_op | source)
XLA Modules:
  0.0 22.6 jit_solution(16626111569763993102)
XLA Ops:
  0.6 1.3 %pick.1 = (f32[40,128]{1,0:T(8,128)S(1)}, f32[40,128]{1,0:T(8,128)S(1)}, f32[40,128]{1,0:T(8,128)S(1)}, f32[40,128]{1,0:T(8,128)S(1)}) custom-call(s32[1]{0:T(128)} %bitcast.info_s, s32[4]{0:T(128)} %bitcast.20, s32[4,32]{1,0:T(4,128)} %bitcast.17, s32[4,32]{1,0:T(4,128)} %bitcast.18, bf16[16,4096]{1,0:T(8,128)(2,1)} %bitcast.13, f32[16,4096]{1,0:T(8,128)} %bitcast.11), custom_call_target="tpu_custom_call" | custom-call | tf_op jit(solution)/shard_map/pick/pallas_call | solution.py:76
  2.0 3.1 %collective-permute-start = (f32[40,128]{1,0:T(8,128)S(1)}, f32[40,128]{1,0:T(8,128)S(1)}, u32[]{:S(2)}, u32[]{:S(2)}) collective-permute-start(f32[40,128]{1,0:T(8,128)S(1)} %get-tuple-element.7), channel_id=1, source_target_pairs={{0,1},{1,0},{2,3},{3,2},{4,5},{5,4},{6,7},{7,6},{8,9},{9,8},{10,11... | collective-permute-start | bytes 61448 | tf_op jit(solution)/shard_map/ppermute | solution.py:161
  5.1 2.6 %collective-permute-start.1 = (f32[40,128]{1,0:T(8,128)S(1)}, f32[40,128]{1,0:T(8,128)S(1)}, u32[]{:S(2)}, u32[]{:S(2)}) collective-permute-start(f32[40,128]{1,0:T(8,128)S(1)} %get-tuple-element.8), channel_id=1, source_target_pairs={{0,2},{1,3},{2,0},{3,1},{4,6},{5,7},{6,4},{7,5},{8,10},{9,11},{10,... | collective-permute-start | bytes 61448 | tf_op jit(solution)/shard_map/ppermute | solution.py:161
  7.7 0.0 collective-permute-start.2
  7.7 0.0 collective-permute-start.3
  7.7 0.0 collective-permute-done.refs_1_
  7.7 0.5 %collective-permute-start.4 = (f32[40,128]{1,0:T(8,128)S(1)}, f32[40,128]{1,0:T(8,128)S(1)}, u32[]{:S(2)}, u32[]{:S(2)}) collective-permute-start(f32[40,128]{1,0:T(8,128)S(1)} %collective-permute-done.refs_1_), channel_id=1, source_target_pairs={{0,4},{4,0},{8,12},{12,8},{16,20},{20,16},{24,28},{28,24},{1,5},{5... | collective-permute-start | bytes 61448 | tf_op jit(solution)/shard_map/ppermute | solution.py:161
  8.2 1.8 %collective-permute-done.1.refs_2_ = f32[40,128]{1,0:T(8,128)S(1)} collective-permute-done((f32[40,128]{1,0:T(8,128)S(1)}, f32[40,128]{1,0:T(8,128)S(1)}, u32[]{:S(2)}, u32[]{:S(2)}) %collective-permute-start.1) | collective-permute-done | bytes 20512 | tf_op jit(solution)/shard_map/ppermute | solution.py:161
  10.0 0.0 collective-permute-start.5
  10.0 3.3 %collective-permute-done.2.refs_3_ = f32[40,128]{1,0:T(8,128)S(1)} collective-permute-done((f32[40,128]{1,0:T(8,128)S(1)}, f32[40,128]{1,0:T(8,128)S(1)}, u32[]{:S(2)}, u32[]{:S(2)}) %collective-permute-start.2) | collective-permute-done | bytes 20512 | tf_op jit(solution)/shard_map/ppermute | solution.py:161
  13.3 0.0 collective-permute-start.6
  13.3 0.0 collective-permute-done.3.refs_4_
  13.3 0.0 collective-permute-done.4.refs_5_
  13.3 0.0 collective-permute-done.5.refs_6_
  13.3 1.2 %collective-permute-done.6.refs_7_ = f32[40,128]{1,0:T(8,128)S(1)} collective-permute-done((f32[40,128]{1,0:T(8,128)S(1)}, f32[40,128]{1,0:T(8,128)S(1)}, u32[]{:S(2)}, u32[]{:S(2)}) %collective-permute-start.6) | collective-permute-done | bytes 20512 | tf_op jit(solution)/shard_map/ppermute | solution.py:161
  14.5 0.2 merge.1
  14.7 2.5 %collective-permute-start.9 = (f32[128,128]{1,0:T(8,128)S(1)}, f32[128,128]{1,0:T(8,128)S(1)}, u32[]{:S(2)}, u32[]{:S(2)}) collective-permute-start(f32[128,128]{1,0:T(8,128)S(1)} %merge.1), channel_id=1, source_target_pairs={{0,24},{4,28},{8,16},{12,20},{16,8},{20,12},{24,0},{28,4},{1,25},{... | collective-permute-start | bytes 196616 | tf_op jit(solution)/shard_map/ppermute | solution.py:161
  17.2 0.5 %collective-permute-start.8 = (f32[128,128]{1,0:T(8,128)S(1)}, f32[128,128]{1,0:T(8,128)S(1)}, u32[]{:S(2)}, u32[]{:S(2)}) collective-permute-start(f32[128,128]{1,0:T(8,128)S(1)} %merge.1), channel_id=1, source_target_pairs={{0,16},{4,20},{8,24},{12,28},{16,0},{20,4},{24,8},{28,12},{1,17},{... | collective-permute-start | bytes 196616 | tf_op jit(solution)/shard_map/ppermute | solution.py:161
  17.7 0.5 %collective-permute-start.7 = (f32[128,128]{1,0:T(8,128)S(1)}, f32[128,128]{1,0:T(8,128)S(1)}, u32[]{:S(2)}, u32[]{:S(2)}) collective-permute-start(f32[128,128]{1,0:T(8,128)S(1)} %merge.1), channel_id=1, source_target_pairs={{0,8},{4,12},{8,0},{12,4},{16,24},{20,28},{24,16},{28,20},{1,9},{5... | collective-permute-start | bytes 196616 | tf_op jit(solution)/shard_map/ppermute | solution.py:161
  18.2 2.6 %keep.1 = f32[16,4096]{1,0:T(8,128)} custom-call(s32[4]{0:T(128)} %bitcast.21, s32[4,32]{1,0:T(4,128)} %bitcast.19, bf16[16,4096]{1,0:T(8,128)(2,1)} %bitcast.14, f32[16,4096]{1,0:T(8,128)} %bitcast.12), custom_call_target="tpu_custom_call" | custom-call | flops 10000000 | bytes 1000000 | tf_op jit(solution)/shard_map/keep/pallas_call | solution.py:112
  20.8 0.0 collective-permute-done.9
  20.8 0.6 %collective-permute-done.8 = f32[128,128]{1,0:T(8,128)S(1)} collective-permute-done((f32[128,128]{1,0:T(8,128)S(1)}, f32[128,128]{1,0:T(8,128)S(1)}, u32[]{:S(2)}, u32[]{:S(2)}) %collective-permute-start.8) | collective-permute-done | bytes 65568 | tf_op jit(solution)/shard_map/ppermute | solution.py:161
  21.4 0.5 %collective-permute-done.7 = f32[128,128]{1,0:T(8,128)S(1)} collective-permute-done((f32[128,128]{1,0:T(8,128)S(1)}, f32[128,128]{1,0:T(8,128)S(1)}, u32[]{:S(2)}, u32[]{:S(2)}) %collective-permute-start.7) | collective-permute-done | bytes 65568 | tf_op jit(solution)/shard_map/ppermute | solution.py:161
  22.0 0.6 %add_multiply_fusion = f32[128,128]{1,0:T(8,128)} fusion(f32[128,128]{1,0:T(8,128)S(1)} %collective-permute-done.9, f32[128,128]{1,0:T(8,128)S(1)} %collective-permute-done.8, f32[128,128]{1,0:T(8,128)S(1)} %merge.1, f32[128,128]{1,0:T(8,128)S(1)} %collective-permute-done.7), kind=kLoop, calls=%fused_computation | loop fusion | flops 65536 | bytes 327680 | tf_op jit(solution)/shard_map/div | solution.py:197
Async XLA Ops:
  2.0 5.7 %collective-permute-start = (f32[40,128]{1,0:T(8,128)S(1)}, f32[40,128]{1,0:T(8,128)S(1)}, u32[]{:S(2)}, u32[]{:S(2)}) collective-permute-start(f32[40,128]{1,0:T(8,128)S(1)} %get-tuple-element.7), channel_id=1, source_target_pairs={{0,1},{1,0},{2,3},{3,2},{4,5},{5,4},{6,7},{7,6},{8,9},{9,8},{10,11... | collective-permute-start | bytes 61448 | tf_op jit(solution)/shard_map/ppermute | solution.py:161
  5.1 4.9 %collective-permute-start.1 = (f32[40,128]{1,0:T(8,128)S(1)}, f32[40,128]{1,0:T(8,128)S(1)}, u32[]{:S(2)}, u32[]{:S(2)}) collective-permute-start(f32[40,128]{1,0:T(8,128)S(1)} %get-tuple-element.8), channel_id=1, source_target_pairs={{0,2},{1,3},{2,0},{3,1},{4,6},{5,7},{6,4},{7,5},{8,10},{9,11},{10,... | collective-permute-start | bytes 61448 | tf_op jit(solution)/shard_map/ppermute | solution.py:161
  7.7 5.6 %collective-permute-start.2 = (f32[40,128]{1,0:T(8,128)S(1)}, f32[40,128]{1,0:T(8,128)S(1)}, u32[]{:S(2)}, u32[]{:S(2)}) collective-permute-start(f32[40,128]{1,0:T(8,128)S(1)} %get-tuple-element.9), channel_id=1, source_target_pairs={{0,3},{1,2},{2,1},{3,0},{4,7},{5,6},{6,5},{7,4},{8,11},{9,10},{10,... | collective-permute-start | bytes 61448 | tf_op jit(solution)/shard_map/ppermute | solution.py:161
  7.7 5.6 %collective-permute-start.3 = (f32[40,128]{1,0:T(8,128)S(1)}, f32[40,128]{1,0:T(8,128)S(1)}, u32[]{:S(2)}, u32[]{:S(2)}) collective-permute-start(f32[40,128]{1,0:T(8,128)S(1)} %get-tuple-element.6.refs_0_), channel_id=1, source_target_pairs={{0,4},{4,0},{8,12},{12,8},{16,20},{20,16},{24,28},{28,24},{1,5},{5... | collective-permute-start | bytes 61448 | tf_op jit(solution)/shard_map/ppermute | solution.py:161
  7.7 5.6 %collective-permute-start.4 = (f32[40,128]{1,0:T(8,128)S(1)}, f32[40,128]{1,0:T(8,128)S(1)}, u32[]{:S(2)}, u32[]{:S(2)}) collective-permute-start(f32[40,128]{1,0:T(8,128)S(1)} %collective-permute-done.refs_1_), channel_id=1, source_target_pairs={{0,4},{4,0},{8,12},{12,8},{16,20},{20,16},{24,28},{28,24},{1,5},{5... | collective-permute-start | bytes 61448 | tf_op jit(solution)/shard_map/ppermute | solution.py:161
  10.0 3.3 %collective-permute-start.5 = (f32[40,128]{1,0:T(8,128)S(1)}, f32[40,128]{1,0:T(8,128)S(1)}, u32[]{:S(2)}, u32[]{:S(2)}) collective-permute-start(f32[40,128]{1,0:T(8,128)S(1)} %collective-permute-done.1.refs_2_), channel_id=1, source_target_pairs={{0,4},{4,0},{8,12},{12,8},{16,20},{20,16},{24,28},{28,24},{1,5},{5... | collective-permute-start | bytes 61448 | tf_op jit(solution)/shard_map/ppermute | solution.py:161
  13.3 1.2 %collective-permute-start.6 = (f32[40,128]{1,0:T(8,128)S(1)}, f32[40,128]{1,0:T(8,128)S(1)}, u32[]{:S(2)}, u32[]{:S(2)}) collective-permute-start(f32[40,128]{1,0:T(8,128)S(1)} %collective-permute-done.2.refs_3_), channel_id=1, source_target_pairs={{0,4},{4,0},{8,12},{12,8},{16,20},{20,16},{24,28},{28,24},{1,5},{5... | collective-permute-start | bytes 61448 | tf_op jit(solution)/shard_map/ppermute | solution.py:161
  14.7 6.2 %collective-permute-start.9 = (f32[128,128]{1,0:T(8,128)S(1)}, f32[128,128]{1,0:T(8,128)S(1)}, u32[]{:S(2)}, u32[]{:S(2)}) collective-permute-start(f32[128,128]{1,0:T(8,128)S(1)} %merge.1), channel_id=1, source_target_pairs={{0,24},{4,28},{8,16},{12,20},{16,8},{20,12},{24,0},{28,4},{1,25},{... | collective-permute-start | bytes 196616 | tf_op jit(solution)/shard_map/ppermute | solution.py:161
  17.2 4.3 %collective-permute-start.8 = (f32[128,128]{1,0:T(8,128)S(1)}, f32[128,128]{1,0:T(8,128)S(1)}, u32[]{:S(2)}, u32[]{:S(2)}) collective-permute-start(f32[128,128]{1,0:T(8,128)S(1)} %merge.1), channel_id=1, source_target_pairs={{0,16},{4,20},{8,24},{12,28},{16,0},{20,4},{24,8},{28,12},{1,17},{... | collective-permute-start | bytes 196616 | tf_op jit(solution)/shard_map/ppermute | solution.py:161
  17.7 4.3 %collective-permute-start.7 = (f32[128,128]{1,0:T(8,128)S(1)}, f32[128,128]{1,0:T(8,128)S(1)}, u32[]{:S(2)}, u32[]{:S(2)}) collective-permute-start(f32[128,128]{1,0:T(8,128)S(1)} %merge.1), channel_id=1, source_target_pairs={{0,8},{4,12},{8,0},{12,4},{16,24},{20,28},{24,16},{28,20},{1,9},{5... | collective-permute-start | bytes 196616 | tf_op jit(solution)/shard_map/ppermute | solution.py:161
